TPU v7x, 32 devices: a whole 2x2x4 slice. The times are simulated.
32 devices in a mesh: dp: 8 (over z, y), mp: 4 (over x, core).
Axes of the slice: x: 2, y: 2, z: 4, core: 2. Of those that a mesh axis runs over, the one named last changes fastest.
Arguments:
- tokens: bfloat16 [8, 1024, 1280], P('dp', 'mp'), may hold values from -6 to 6
- sizes: float32 [8, 1024], P('dp'), may hold values from 1 to 8
- ln1_gain: float32 [1280], replicated, may hold values from 0.25 to 1.75
- qkv_weight: bfloat16 [3, 1280, 1280], P(None, 'dp', 'mp'), may hold values from -0.15625 to 0.15625
- proj_weight: bfloat16 [1280, 1280], P('mp', 'dp'), may hold values from -0.15625 to 0.15625
- ln2_gain: float32 [1280], replicated, may hold values from 0.25 to 1.75
- fc1_weight: bfloat16 [1280, 5120], P('dp', 'mp'), may hold values from -0.15625 to 0.15625
- fc1_bias: float32 [5120], P('mp'), may hold values from -3 to 3
- fc2_weight: bfloat16 [5120, 1280], P('mp', 'dp'), may hold values from -0.078125 to 0.078125
- pair_source: int32 [8, 16], P('dp'), may hold values from 0 to 1022, as said below
- pair_target: int32 [8, 16], P('dp'), may hold values from 1 to 1023, as said below
- kept_order: int32 [8, 1008], P('dp'), may hold values from 0 to 1023, as said below
Outputs:
- merged_out: bfloat16 [8, 1008, 1280], P('dp', 'mp')
Inputs may be any that keep to these rules, and one draw needn't show every extreme that they name: `pair_source`: in each image the 16 entries are distinct even token indices. `pair_target`: odd token indices; several sources may join the same target. `kept_order`: in each image every token index that is not in pair_source appears exactly once.
All inputs are finite; a program needn't handle non-finite values.
Results may differ from a plain program's by a relative error of at most 0.017.
Values may be sent and summed in bfloat16 or wider, within the bound.
A program may use at most 64 MiB of HBM per device.

v0:
```python
import math
import jax
import jax.numpy as jnp
from jax import lax
from jax.sharding import PartitionSpec as P

D = 1280
HEADS = 16


def layer_norm(values, gain):
    center = values - jnp.mean(values, axis=-1, keepdims=True)
    spread = jnp.mean(center * center, axis=-1, keepdims=True)
    return center * lax.rsqrt(spread + 1e-06) * gain


def merge_rows(total, order_rows, source_ids, target_ids):
    kept_rows = jnp.take_along_axis(total, order_rows[:, :, None], axis=1)
    source_rows = jnp.take_along_axis(total, source_ids[:, :, None], axis=1)
    joins = (order_rows[:, :, None] == target_ids[:, None, :]).astype(jnp.float32)
    return kept_rows + jnp.einsum(
        "icr,ird->icd", joins, source_rows, precision=lax.Precision.HIGHEST
    )


def shards(
    tokens,
    sizes,
    ln1_gain,
    qkv_weight,
    proj_weight,
    ln2_gain,
    fc1_weight,
    fc1_bias,
    fc2_weight,
    pair_source,
    pair_target,
    kept_order,
):
    images, own_tokens, width = tokens.shape
    length = sizes.shape[1]
    kept_total = kept_order.shape[1]
    devices_mp = lax.axis_size("mp")
    own_start = lax.axis_index("mp") * own_tokens
    head_size = D // HEADS
    base = tokens.astype(jnp.float32)
    normed = layer_norm(base, ln1_gain).astype(jnp.bfloat16)
    whole = lax.all_gather(normed, "mp", axis=1, tiled=True)
    local_width = qkv_weight.shape[2]
    columns = whole
    projected = jnp.einsum(
        "ind,cdf->cinf",
        columns,
        lax.all_gather(qkv_weight, "dp", axis=1, tiled=True),
        preferred_element_type=jnp.float32,
    ).astype(jnp.bfloat16)
    local_heads = local_width // head_size
    shaped = projected.reshape(3, images, length, local_heads, head_size)
    queries = shaped[0]
    keys_all = shaped[1]
    values_all = shaped[2]
    size_bias = jnp.log(sizes)[:, None, None, :]
    block = min(512, length)
    outputs = []
    for begin in range(0, length, block):
        scores = (
            jnp.einsum(
                "iqhe,ikhe->ihqk",
                queries[:, begin : begin + block],
                keys_all,
                preferred_element_type=jnp.float32,
            )
            / math.sqrt(head_size)
            + size_bias
        )
        weights = jax.nn.softmax(scores, axis=-1).astype(jnp.bfloat16)
        attended_block = jnp.einsum(
            "ihqk,ikhe->iqhe", weights, values_all, preferred_element_type=jnp.float32
        )
        outputs.append(attended_block.astype(jnp.bfloat16).reshape(images, block, local_width))
    attended = jnp.concatenate(outputs, axis=1)
    branch = jnp.einsum(
        "ind,de->ine",
        attended,
        lax.all_gather(proj_weight, "dp", axis=1, tiled=True),
        preferred_element_type=jnp.float32,
    )
    weighted = sizes[:, :, None] * branch
    own_sizes = lax.dynamic_slice_in_dim(sizes, own_start, own_tokens, 1)
    own_weighted = own_sizes[:, :, None] * base
    local_total = lax.dynamic_update_slice_in_dim(
        weighted,
        lax.dynamic_slice_in_dim(weighted, own_start, own_tokens, 1) + own_weighted,
        own_start,
        1,
    )
    merged_count = kept_total // devices_mp
    own_order = lax.dynamic_slice_in_dim(
        kept_order, lax.axis_index("mp") * merged_count, merged_count, 1
    )
    scattered = lax.psum_scatter(
        jnp.transpose(
            merge_rows(local_total, kept_order, pair_source, pair_target), (1, 0, 2)
        ).astype(jnp.bfloat16),
        "mp",
        scatter_dimension=0,
        tiled=True,
    ).astype(jnp.float32)
    numerator = jnp.transpose(scattered, (1, 0, 2))
    merged_size = merge_rows(sizes[:, :, None], own_order, pair_source, pair_target)
    merged = numerator / merged_size
    normed_two = layer_norm(merged, ln2_gain).astype(jnp.bfloat16)
    gathered = lax.all_gather(normed_two, "mp", axis=1, tiled=True)
    columns = gathered
    hidden_sum = jnp.einsum(
        "imd,df->imf",
        columns,
        lax.all_gather(fc1_weight, "dp", axis=0, tiled=True),
        preferred_element_type=jnp.float32,
    )
    hidden = jax.nn.gelu(hidden_sum + fc1_bias).astype(jnp.bfloat16)
    partial_out = jnp.einsum(
        "imf,fd->imd",
        hidden,
        lax.all_gather(fc2_weight, "dp", axis=1, tiled=True),
        preferred_element_type=jnp.float32,
    )
    mlp_part = lax.psum_scatter(
        partial_out.astype(jnp.bfloat16), "mp", scatter_dimension=1, tiled=True
    ).astype(jnp.float32)
    return (merged + mlp_part).astype(jnp.bfloat16)


def solution(mesh):
    return jax.shard_map(
        shards,
        mesh=mesh,
        in_specs=(
            P("dp", "mp", None),
            P("dp", None),
            P(),
            P(None, "dp", "mp"),
            P("mp", "dp"),
            P(),
            P("dp", "mp"),
            P("mp"),
            P("mp", "dp"),
            P("dp", None),
            P("dp", None),
            P("dp", None),
        ),
        out_specs=P("dp", "mp", None),
        check_vma=False,
    )
```

profile of v0, /device:TPU:1, one launch (start us, length us, event | category | flops | bytes accessed | tf_op | source)
XLA Modules:
  0.0 317.7 jit_solution(4380768634615341311)
XLA Ops:
  6.5 0.0 all-gather.6.cloned.1.call-start
  6.6 1.3 convert_reduce_fusion
  7.9 1.4 fusion.30
  9.3 2.2 fusion.32
  11.5 0.0 all-gather.6.cloned.1.call-update
  11.6 0.0 all-gather.8.cloned.1.call-start
  11.6 0.7 all-gather.8.cloned.1.call-update
  12.3 0.0 all-gather.12.cloned.1.call-start
  12.4 0.7 all-gather.12.cloned.1.call-update
  13.0 0.0 all-gather.14.cloned.1.call-start
  13.1 0.5 all-gather.14.cloned.1.call-update
  13.6 0.0 all-gather.10.cloned.1.call-start
  13.8 28.3 %all_gather.20 = bf16[320,1280]{0,1:T(8,128)(2,1)S(1)} all-gather(bf16[320,160]{0,1:T(8,128)(2,1)S(1)} %copy-done.2), channel_id=1, replica_groups=mesh['dp'=8,'mp'=4] {'dp'}, dimensions={1}, use_global_device_ids=true | all-gather | bytes 921600 | tf_op jit(solution)/shard_map/all_gather | solution.py:85
  42.1 0.1 compare_select_fusion.2
  42.2 0.6 gather_fusion.3
  42.8 1.4 gather_fusion.2
  44.2 0.2 fusion.56
  44.4 53.4 %all-gather.8.cloned.1.call-done = bf16[3,1280,320]{2,1,0:T(8,128)(2,1)} async-done(((bf16[3,160,320]{2,1,0:T(8,128)(2,1)}), bf16[3,1280,320]{2,1,0:T(8,128)(2,1)}) %all-gather.8.cloned.1.call-update) | async-done | bytes 2457616 | tf_op jit(solution)/shard_map/all_gather | solution.py:54
  97.8 5.4 %convert_bitcast_fusion = bf16[3,1,1024,320]{2,3,0,1:T(8,128)(2,1)S(1)} fusion(bf16[3,1280,320]{2,1,0:T(8,128)(2,1)} %all-gather.8.cloned.1.call-done, bf16[1,1024,1280]{2,1,0:T(8,128)(2,1)} %all-gather.6.cloned.1.call-done), kind=kOutput, calls=%fused_computation.38 | convolution fusion | flops 2517565440 | bytes 7045120 | tf_op jit(solution)/shard_map/ind,cdf->cinf/dot_general | solution.py:51
  103.2 0.2 fusion.78
  103.3 4.9 %fusion.80 = (f32[4,512]{1,0:T(4,128)S(1)}, f32[4,512,1024]{2,1,0:T(8,128)}) fusion(f32[1024]{0:T(1024)S(1)} %bitcast.179, bf16[1024,4,80]{0,2,1:T(8,128)(2,1)S(1)} %bitcast.170, bf16[1,1024,4,80]{1,3,2,0:T(8,128)(2,1)S(1)} %bitcast.168), kind=kOutput, calls=%fused_computation.120 | convolution fusion | flops 343933952 | bytes 9383936 | tf_op jit(solution)/shard_map/sub | solution.py:76
  108.2 4.9 %fusion.79 = (f32[4,512]{1,0:T(4,128)S(1)}, f32[4,512,1024]{2,1,0:T(8,128)}) fusion(f32[1024]{0:T(1024)S(1)} %bitcast.180, bf16[1024,4,80]{0,2,1:T(8,128)(2,1)S(1)} %bitcast.171, bf16[1,1024,4,80]{1,3,2,0:T(8,128)(2,1)S(1)} %bitcast.169), kind=kOutput, calls=%fused_computation.119 | convolution fusion | flops 343933952 | bytes 9383936 | tf_op jit(solution)/shard_map/sub | solution.py:76
  113.0 5.1 %fusion.37 = bf16[4,80,512]{2,1,0:T(8,128)(2,1)S(1)} fusion(bf16[1024,4,80]{0,2,1:T(8,128)(2,1)S(1)} %bitcast.166, f32[4,512,1024]{2,1,0:T(8,128)} %get-tuple-element.13, f32[4,512]{1,0:T(4,128)S(1)} %get-tuple-element.12), kind=kOutput, calls=%fused_computation.55 | convolution fusion | flops 339902464 | bytes 9379840 | tf_op jit(solution)/shard_map/ihqk,ikhe->iqhe/dot_general | solution.py:77
  118.1 0.8 copy-done.9
  118.9 1.7 fusion.36
  120.6 4.0 %convolution_multiply_fusion = f32[1024,1280]{1,0:T(8,128)} fusion(bf16[320,1280]{0,1:T(8,128)(2,1)S(1)} %all_gather.20, f32[1024]{0:T(1024)S(1)} %bitcast.165, bf16[1,512,320]{1,2,0:T(8,128)(2,1)S(1)} %bitcast.173, bf16[1,512,320]{1,2,0:T(8,128)(2,1)S(1)} %bitcast.172), kind=kOutput, calls=%fused_computation.24 | convolution fusion | flops 841482240 | bytes 6721536 | tf_op jit(solution)/shard_map/ind,de->ine/dot_general | solution.py:82
  124.6 1.4 constant_dynamic-slice_fusion.2
  126.0 1.3 fusion.35
  127.3 3.1 gather_fusion.1
  130.5 9.7 %gather_fusion = f32[1008,1280]{1,0:T(8,128)} fusion(f32[1024,1280]{1,0:T(8,128)} %fusion.35, s32[1024]{0:T(1024)S(1)} %pad_clamp_fusion.2), kind=kCustom, calls=%fused_computation | custom fusion | bytes 10325952 | tf_op jit(solution)/shard_map/jit(take_along_axis)/gather | solution.py:18
  140.1 5.1 %fusion.21 = bf16[1008,1,1280]{2,0,1:T(8,128)(2,1)S(1)} fusion(f32[1008,1280]{1,0:T(8,128)} %gather_fusion, pred[1008]{0:T(1024)(128)(4,1)S(1)} %compare_and_fusion, f32[16,1280]{1,0:T(8,128)S(1)} %gather_fusion.1, pred[16]{0:T(512)(128)(4,1)S(1)} %compare_and_fusion.1, s32[1008]{0:T(1024)S(1)} %bitcast.175, s32[16]{0:T(128)S(1)} %bitcast.185), kind=kOutput, calls=%fused_computation.33 | convolution fusion | flops 251633408 | bytes 7828480 | tf_op jit(solution)/shard_map/icr,ird->icd/dot_general | solution.py:21
  145.2 27.6 %fusion = bf16[256,1280]{1,0:T(8,128)(2,1)S(1)} fusion(bf16[1008,1,1280]{2,0,1:T(8,128)(2,1)S(1)} %fusion.21), kind=kCustom, calls=%all-reduce-scatter | all-reduce-scatter fusion | flops 1310721 | bytes 3236352
  172.8 4.4 %collective-permute-start = (bf16[12,1280]{1,0:T(8,128)(2,1)S(1)}, bf16[12,1280]{1,0:T(8,128)(2,1)S(1)}, u32[]{:S(2)}, u32[]{:S(2)}) collective-permute-start(bf16[12,1280]{1,0:T(8,128)(2,1)S(1)} %slice.36), channel_id=1, source_target_pairs={{0,1},{1,2},{2,3},{4,5},{5,6},{6,7},{8,9},{9,10},{10,11},{12,13},{... | collective-permute-start | bytes 92168
  177.2 0.6 dynamic-slice.10
  178.5 1.1 concatenate.4
  179.6 0.4 fusion.46
  180.0 0.5 multiply_reduce_fusion
  180.5 0.4 multiply_convert_fusion
  180.9 2.1 copy.14
  183.0 0.0 all-gather.12.cloned.1.call-done
  183.1 39.2 %all-gather.14.cloned.1.call-done = bf16[1280,1280]{0,1:T(8,128)(2,1)} async-done(((bf16[1280,160]{0,1:T(8,128)(2,1)}), bf16[1280,1280]{0,1:T(8,128)(2,1)}) %all-gather.14.cloned.1.call-update) | async-done | bytes 3276816 | tf_op jit(solution)/shard_map/all_gather | solution.py:125
  222.2 42.2 %all-gather.10.cloned.1.call-done = bf16[1,1008,1280]{2,0,1:T(2,128)(2,1)} async-done(((bf16[1,252,1280]{2,0,1:T(2,128)(2,1)}), bf16[1,1008,1280]{2,0,1:T(2,128)(2,1)}) %all-gather.10.cloned.1.call-update) | async-done | bytes 2580496 | tf_op jit(solution)/shard_map/all_gather | solution.py:113
  264.5 12.8 %fusion.20 = bf16[1,1008,1280]{2,1,0:T(8,128)(2,1)} fusion(bf16[1280,1280]{0,1:T(8,128)(2,1)} %all-gather.14.cloned.1.call-done, bf16[1280,1280]{1,0:T(8,128)(2,1)} %all-gather.12.cloned.1.call-done, bf16[1,1008,1280]{2,0,1:T(2,128)(2,1)} %all-gather.10.cloned.1.call-done, f32[1280]{0:T(1024)S(1)} %copy-done.7), kind=kOutput, calls=%fused_computation.32 | convolution fusion | flops 6620221440 | bytes 11719680 | tf_op jit(solution)/shard_map/imf,fd->imd/dot_general | solution.py:122
  277.3 26.0 %fusion.1 = bf16[256,1280]{1,0:T(8,128)(2,1)S(1)} fusion(bf16[1,1008,1280]{2,1,0:T(8,128)(2,1)} %fusion.20), kind=kCustom, calls=%all-reduce-scatter.1 | all-reduce-scatter fusion | flops 1310721 | bytes 3236352
  303.4 4.4 %collective-permute-start.1 = (bf16[12,1280]{1,0:T(8,128)(2,1)S(1)}, bf16[12,1280]{1,0:T(8,128)(2,1)S(1)}, u32[]{:S(2)}, u32[]{:S(2)}) collective-permute-start(bf16[12,1280]{1,0:T(8,128)(2,1)S(1)} %slice.37), channel_id=1, source_target_pairs={{0,1},{1,2},{2,3},{4,5},{5,6},{6,7},{8,9},{9,10},{10,11},{12,13},{... | collective-permute-start | bytes 92168
  307.8 1.1 collective-permute-done.1
  308.9 1.0 concatenate.5
  309.9 1.3 add_convert_fusion.1
  (38 shorter events, 0.2 us)
Async XLA Ops:
  6.5 7.1 %copy-start.8 = (s32[1,16]{1,0:T(1,128)S(1)}, s32[1,16]{1,0:T(1,128)}, u32[]{:S(2)}) copy-start(s32[1,16]{1,0:T(1,128)} %param.21) | copy-start | bytes 196
  6.5 7.2 %copy-start = (f32[1,1024]{1,0:T(1,128)S(1)}, f32[1,1024]{1,0:T(1,128)}, u32[]{:S(2)}) copy-start(f32[1,1024]{1,0:T(1,128)} %param.13) | copy-start | bytes 12292
  6.5 7.2 %copy-start.2 = (bf16[320,160]{0,1:T(8,128)(2,1)S(1)}, bf16[320,160]{0,1:T(8,128)(2,1)}, u32[]{:S(2)}) copy-start(bf16[320,160]{0,1:T(8,128)(2,1)} %param.16) | copy-start | bytes 307204
  6.5 35.5 %copy-start.3 = (s32[1,1008]{1,0:T(1,128)S(1)}, s32[1,1008]{1,0:T(1,128)}, u32[]{:S(2)}) copy-start(s32[1,1008]{1,0:T(1,128)} %param.23) | copy-start | bytes 12100
  6.5 37.8 %all-gather.6.cloned.1.call-start = ((), (), s32[]{:S(2)}) async-start(), calls=%async_computation | async-start | bytes 3276800 | tf_op jit(solution)/shard_map/all_gather | solution.py:48
  7.9 36.3 %copy-start.5 = (s32[1,16]{1,0:T(1,128)S(1)}, s32[1,16]{1,0:T(1,128)}, u32[]{:S(2)}) copy-start(s32[1,16]{1,0:T(1,128)} %param.22) | copy-start | bytes 196
  11.6 86.2 %all-gather.8.cloned.1.call-start = ((), (), s32[]{:S(2)}) async-start(), calls=%async_computation.1 | async-start | bytes 3317760 | tf_op jit(solution)/shard_map/all_gather | solution.py:54
  12.3 170.7 %all-gather.12.cloned.1.call-start = ((), (), s32[]{:S(2)}) async-start(), calls=%async_computation.3 | async-start | bytes 3686400 | tf_op jit(solution)/shard_map/all_gather | solution.py:118
  13.0 209.2 %all-gather.14.cloned.1.call-start = ((), (), s32[]{:S(2)}) async-start(), calls=%async_computation.4 | async-start | bytes 3686400 | tf_op jit(solution)/shard_map/all_gather | solution.py:125
  13.6 250.8 %all-gather.10.cloned.1.call-start = ((), (), s32[]{:S(2)}) async-start(), calls=%async_computation.2 | async-start | bytes 6451200 | tf_op jit(solution)/shard_map/all_gather | solution.py:113
  113.0 5.9 %copy-start.9 = (f32[4,512,1024]{2,1,0:T(8,128)S(1)}, f32[4,512,1024]{2,1,0:T(8,128)}, u32[]{:S(2)}) copy-start(f32[4,512,1024]{2,1,0:T(8,128)} %get-tuple-element.11) | copy-start | bytes 25165828
  120.6 5.4 %copy-start.1 = (bf16[1,256,1280]{2,1,0:T(8,128)(2,1)S(1)}, bf16[1,256,1280]{2,1,0:T(8,128)(2,1)}, u32[]{:S(2)}) copy-start(bf16[1,256,1280]{2,1,0:T(8,128)(2,1)} %param.12) | copy-start | bytes 1966084
  145.2 32.0 %copy-start.6 = (u32[32]{0:T(128)S(1)}, u32[32]{0:T(128)}, u32[]{:S(2)}) copy-start(u32[32]{0:T(128)} %constant.99) | copy-start | bytes 388
  145.2 35.3 %copy-start.4 = (f32[1280]{0:T(1024)S(1)}, f32[1280]{0:T(1024)}, u32[]{:S(2)}) copy-start(f32[1280]{0:T(1024)} %param.17) | copy-start | bytes 15364
  172.8 5.7 %collective-permute-start = (bf16[12,1280]{1,0:T(8,128)(2,1)S(1)}, bf16[12,1280]{1,0:T(8,128)(2,1)S(1)}, u32[]{:S(2)}, u32[]{:S(2)}) collective-permute-start(bf16[12,1280]{1,0:T(8,128)(2,1)S(1)} %slice.36), channel_id=1, source_target_pairs={{0,1},{1,2},{2,3},{4,5},{5,6},{6,7},{8,9},{9,10},{10,11},{12,13},{... | collective-permute-start | bytes 92168
  179.6 84.9 %copy-start.7 = (f32[1280]{0:T(1024)S(1)}, f32[1280]{0:T(1024)}, u32[]{:S(2)}) copy-start(f32[1280]{0:T(1024)} %param.19) | copy-start | bytes 15364
  303.4 5.5 %collective-permute-start.1 = (bf16[12,1280]{1,0:T(8,128)(2,1)S(1)}, bf16[12,1280]{1,0:T(8,128)(2,1)S(1)}, u32[]{:S(2)}, u32[]{:S(2)}) collective-permute-start(bf16[12,1280]{1,0:T(8,128)(2,1)S(1)} %slice.37), channel_id=1, source_target_pairs={{0,1},{1,2},{2,3},{4,5},{5,6},{6,7},{8,9},{9,10},{10,11},{12,13},{... | collective-permute-start | bytes 92168
Sparse Core Ops, SparseCore 0:
  11.7 27.9 all-gather.5
  41.9 55.8 all-gather.7
  100.0 59.9 all-gather.11
  162.0 60.1 all-gather.13
  223.6 40.7 all-gather.9
where the time goes:
time: 318 us
  waiting for transfers between devices  138 us (43%)
  blocking collectives  81.9 us (26%)
  matrix products  44 us (14%)
  local copies, waits for them, and re-layouts  22 us (7%)
  between operations  14.1 us (4%)
  starting transfers between devices  8.96 us (3%)
  other arithmetic  8.93 us (3%)
    unnamed x2, blocking collectives  53.6 us
    all_gather x1, waiting for transfers between devices, shards(): lax.all_gather(qkv_weight, 'dp', axis=1, tiled=True)  53.4 us
    all_gather x1, waiting for transfers between devices, shards(): gathered = lax.all_gather(normed_two, 'mp', axis=1, tiled=True)  42.2 us
    all_gather x1, waiting for transfers between devices, shards(): lax.all_gather(fc2_weight, 'dp', axis=1, tiled=True)  39.2 us
    all_gather x1, blocking collectives, shards(): lax.all_gather(proj_weight, 'dp', axis=1, tiled=True)  28.3 us
    dot_general x1, matrix products, shards(): jnp.einsum('imf,fd->imd', hidden, lax.all_gather(fc2_weight, 'dp', axis=1...  12.8 us
    gather x2, local copies, waits for them, and re-layouts, merge_rows(): kept_rows = jnp.take_along_axis(total, order_rows[:, :, None], axis=1)  11 us
    sub x2, matrix products, shards(): weights = jax.nn.softmax(scores, axis=-1).astype(jnp.bfloat16)  9.7 us
  transfers between devices with their start and end apart: 7, of which 4 were waited for; matrix products, arithmetic and copies ran while one was open for 26% of the time, Pallas kernels for 0%

commit v1 on v0

--- a/solution.py
+++ b/solution.py
@@ -48,11 +48,39 @@
     whole = lax.all_gather(normed, "mp", axis=1, tiled=True)
     local_width = qkv_weight.shape[2]
     columns = whole
-    projected = jnp.einsum(
-        "ind,cdf->cinf",
-        columns,
-        lax.all_gather(qkv_weight, "dp", axis=1, tiled=True),
-        preferred_element_type=jnp.float32,
+
+    def expand_the_ladders(inp, peer_axis, s0):
+        val, v_now, oldest = (
+            jax.lax.axis_size(peer_axis),
+            jax.lax.axis_index(peer_axis),
+            inp.shape[1],
+        )
+        value_now = map(lambda to_i: (to_i, (to_i + 1) % val), range(val))
+        grid = list(value_now)
+        found_now = range(val)
+        windows = list(map(lambda to_i: (to_i, (to_i - 1) % val), found_now))
+        last = val // 2
+        m_next = carry = inp
+        arr_now = s0(inp, v_now * oldest)
+        at = 1
+        while at < last + 1:
+            m_next = jax.lax.ppermute(m_next, axis_name=peer_axis, perm=grid)
+            if at < val - last:
+                carry = jax.lax.ppermute(carry, axis_name=peer_axis, perm=windows)
+                arr_now = arr_now + s0(carry, (v_now + at) % val * oldest)
+            arr_now = arr_now + s0(m_next, (v_now - at) % val * oldest)
+            at = at + 1
+        return arr_now
+
+    projected = expand_the_ladders(
+        qkv_weight,
+        "dp",
+        lambda shard, start: jnp.einsum(
+            "ind,cdf->cinf",
+            lax.dynamic_slice_in_dim(columns, start, shard.shape[1], axis=2),
+            shard,
+            preferred_element_type=jnp.float32,
+        ),
     ).astype(jnp.bfloat16)
     local_heads = local_width // head_size
     shaped = projected.reshape(3, images, length, local_heads, head_size)

time: 318 us -> 307 us (0.965)
  waiting for transfers between devices: 138 us -> 77.6 us
  starting transfers between devices: 8.96 us -> 25.1 us
  blocking collectives: 81.9 us -> 97.4 us
  matrix products: 44 us -> 59 us
    all_gather x1 -> x0, waiting for transfers between devices: 53.4 us -> none  [shards(): lax.all_gather(qkv_weight, 'dp', axis=1, tiled=True)]
    all_gather x1, waiting for transfers between devices: 39.2 us -> 0.02 us  [shards(): lax.all_gather(fc2_weight, 'dp', axis=1, tiled=True)]
    ppermute x0 -> x7, waiting for transfers between devices: none -> 35.9 us  [the longest x4 21.1 us: expand_the_ladders(): m_next = jax.lax.ppermute(m_next, axis_name=peer_axis, perm=grid)]
    ppermute x0 -> x7, starting transfers between devices: none -> 16.1 us  [the longest x3 9.61 us: expand_the_ladders(): carry = jax.lax.ppermute(carry, axis_name=peer_axis, perm=windows)]
    dot_general x1 -> x8, matrix products: 5.38 us -> 20 us  [shards(): jnp.einsum('ind,cdf->cinf', lax.dynamic_slice_in_dim(columns, start, shar...]
    all_gather x1, blocking collectives: 28.3 us -> 39 us  [shards(): lax.all_gather(proj_weight, 'dp', axis=1, tiled=True)]
    unnamed x2, blocking collectives: 53.6 us -> 58.4 us
  transfers between devices with their start and end apart: 7 -> 13, of which waited for: 4 -> 5; matrix products, arithmetic and copies ran while one was open for 26% -> 34% of each run, Pallas kernels for 0% -> 0%
where the time goes in v1:
time: 307 us; the launch traced here: 306 us
  blocking collectives  97.4 us (32%)
  waiting for transfers between devices  77.6 us (25%)
  matrix products  59 us (19%)
  starting transfers between devices  25.1 us (8%)
  local copies, waits for them, and re-layouts  23.9 us (8%)
  between operations  14.4 us (5%)
  other arithmetic  8.89 us (3%)
    unnamed x2, blocking collectives  58.4 us
    all_gather x1, waiting for transfers between devices, shards(): gathered = lax.all_gather(normed_two, 'mp', axis=1, tiled=True)  39.8 us
    all_gather x1, blocking collectives, shards(): lax.all_gather(proj_weight, 'dp', axis=1, tiled=True)  39 us
    ppermute x4, waiting for transfers between devices, expand_the_ladders(): m_next = jax.lax.ppermute(m_next, axis_name=peer_axis, perm=grid)  21.1 us
    dot_general x8, matrix products, shards(): jnp.einsum('ind,cdf->cinf', lax.dynamic_slice_in_dim(columns, start, shar...  20 us
    ppermute x3, waiting for transfers between devices, expand_the_ladders(): carry = jax.lax.ppermute(carry, axis_name=peer_axis, perm=windows)  14.8 us
    dot_general x1, matrix products, shards(): jnp.einsum('imf,fd->imd', hidden, lax.all_gather(fc2_weight, 'dp', axis=1...  12.9 us
    gather x2, local copies, waits for them, and re-layouts, merge_rows(): kept_rows = jnp.take_along_axis(total, order_rows[:, :, None], axis=1)  10.9 us
  transfers between devices with their start and end apart: 13, of which 5 were waited for; matrix products, arithmetic and copies ran while one was open for 34% of the time, Pallas kernels for 0%

profile of v1, /device:TPU:1, one launch (start us, length us, event | category | flops | bytes accessed | tf_op | source)
XLA Modules:
  0.0 306.2 jit_solution(3818731294387938143)
XLA Ops:
  6.6 1.3 convert_reduce_fusion
  7.9 1.4 fusion.27
  9.3 2.2 fusion.29
  11.6 0.7 all-gather.11.cloned.1.call-update
  12.4 2.1 collective-permute-start.1
  14.5 3.1 %collective-permute-start = (bf16[3,160,320]{2,1,0:T(8,128)(2,1)}, bf16[3,160,320]{2,1,0:T(8,128)(2,1)S(1)}, u32[]{:S(2)}, u32[]{:S(2)}) collective-permute-start(bf16[3,160,320]{2,1,0:T(8,128)(2,1)} %param.15), channel_id=1, source_target_pairs={{0,28},{4,0},{8,4},{12,8},{16,12},{20,16},{24,20},{28,24},{1,29},{... | collective-permute-start | bytes 921608 | tf_op jit(solution)/shard_map/ppermute | solution.py:69
  18.0 0.6 gather_fusion.3
  18.6 1.4 gather_fusion.2
  20.3 9.7 %collective-permute-done.1 = bf16[3,160,320]{2,1,0:T(8,128)(2,1)S(1)} collective-permute-done((bf16[3,160,320]{2,1,0:T(8,128)(2,1)}, bf16[3,160,320]{2,1,0:T(8,128)(2,1)S(1)}, u32[]{:S(2)}, u32[]{:S(2)}) %collective-permute-start.1) | collective-permute-done | bytes 307232 | tf_op jit(solution)/shard_map/ppermute | solution.py:67
  30.0 2.2 collective-permute-start.3
  32.2 3.1 %collective-permute-start.2 = (bf16[3,160,320]{2,1,0:T(8,128)(2,1)S(1)}, bf16[3,160,320]{2,1,0:T(8,128)(2,1)}, u32[]{:S(2)}, u32[]{:S(2)}) collective-permute-start(bf16[3,160,320]{2,1,0:T(8,128)(2,1)S(1)} %collective-permute-done), channel_id=1, source_target_pairs={{0,28},{4,0},{8,4},{12,8},{16,12},{20,16},{24,20},{28,24},{1,29},{... | collective-permute-start | bytes 921608 | tf_op jit(solution)/shard_map/ppermute | solution.py:69
  35.3 11.4 %collective-permute-done.3 = bf16[3,160,320]{2,1,0:T(8,128)(2,1)S(1)} collective-permute-done((bf16[3,160,320]{2,1,0:T(8,128)(2,1)S(1)}, bf16[3,160,320]{2,1,0:T(8,128)(2,1)S(1)}, u32[]{:S(2)}, u32[]{:S(2)}) %collective-permute-start.3) | collective-permute-done | bytes 307232 | tf_op jit(solution)/shard_map/ppermute | solution.py:67
  46.7 2.2 collective-permute-start.5
  48.9 39.0 %all_gather.16 = bf16[320,1280]{0,1:T(8,128)(2,1)S(1)} all-gather(bf16[320,160]{0,1:T(8,128)(2,1)S(1)} %copy-done.6), channel_id=1, replica_groups=mesh['dp'=8,'mp'=4] {'dp'}, dimensions={1}, use_global_device_ids=true | all-gather | bytes 921600 | tf_op jit(solution)/shard_map/all_gather | solution.py:113
  87.9 3.4 %collective-permute-start.4 = (bf16[3,160,320]{2,1,0:T(8,128)(2,1)}, bf16[3,160,320]{2,1,0:T(8,128)(2,1)}, u32[]{:S(2)}, u32[]{:S(2)}) collective-permute-start(bf16[3,160,320]{2,1,0:T(8,128)(2,1)} %collective-permute-done.2), channel_id=1, source_target_pairs={{0,28},{4,0},{8,4},{12,8},{16,12},{20,16},{24,20},{28,24},{1,29},{... | collective-permute-start | bytes 921608 | tf_op jit(solution)/shard_map/ppermute | solution.py:69
  91.3 2.2 fusion.45
  93.5 0.8 fusion.49
  94.4 1.8 fusion.51
  96.2 0.8 fusion.53
  97.2 0.8 fusion.55
  98.0 2.7 fusion.57
  100.7 14.8 %collective-permute-done.4 = bf16[3,160,320]{2,1,0:T(8,128)(2,1)} collective-permute-done((bf16[3,160,320]{2,1,0:T(8,128)(2,1)}, bf16[3,160,320]{2,1,0:T(8,128)(2,1)}, u32[]{:S(2)}, u32[]{:S(2)}) %collective-permute-start.4) | collective-permute-done | bytes 307232 | tf_op jit(solution)/shard_map/ppermute | solution.py:69
  115.5 3.7 %fusion.47 = f32[1024,3,320]{0,2,1:T(8,128)} fusion(bf16[3,160,320]{2,1,0:T(8,128)(2,1)} %collective-permute-done.4, bf16[1,1024,1280]{2,1,0:T(8,128)(2,1)S(1)} %copy-done.2, s32[]{:T(128)S(6)} %select_n.215), kind=kOutput, calls=%fused_computation.65 | convolution fusion | flops 314572800 | bytes 4763652 | tf_op jit(solution)/shard_map/ind,cdf->cinf/dot_general | solution.py:78
  119.2 7.1 %fusion.24 = bf16[3,1,1024,320]{2,3,0,1:T(8,128)(2,1)} fusion(bf16[3,160,320]{2,1,0:T(8,128)(2,1)} %collective-permute-done.6, f32[1024,3,320]{0,2,1:T(8,128)S(1)} %fusion.45, f32[1024,3,320]{0,2,1:T(8,128)} %fusion.47, f32[1024,3,320]{0,2,1:T(8,128)S(1)} %fusion.49, f32[1024,3,320]{0,2,1:T(8,128)S(1)} %fusion.51, f32[1024,3,320]{0,2,1:T(8,128)S(1)} %fusion.53, ...), kind=kOutput, calls=%fused_computation.40 | convolution fusion | flops 322437120 | bytes 30384132 | tf_op jit(solution)/shard_map/ind,cdf->cinf/dot_general | solution.py:78
  126.3 1.6 fusion.106
  127.9 5.0 %fusion.108 = (f32[4,512]{1,0:T(4,128)S(1)}, f32[4,512,1024]{2,1,0:T(8,128)}) fusion(f32[1024]{0:T(1024)S(1)} %bitcast.220, bf16[1024,4,80]{0,2,1:T(8,128)(2,1)S(1)} %bitcast.211, bf16[1,1024,4,80]{1,3,2,0:T(8,128)(2,1)S(1)} %bitcast.209), kind=kOutput, calls=%fused_computation.150 | convolution fusion | flops 343933952 | bytes 9383936 | tf_op jit(solution)/shard_map/sub | solution.py:104
  132.9 4.8 %fusion.107 = (f32[4,512]{1,0:T(4,128)S(1)}, f32[4,512,1024]{2,1,0:T(8,128)}) fusion(f32[1024]{0:T(1024)S(1)} %bitcast.221, bf16[1024,4,80]{0,2,1:T(8,128)(2,1)S(1)} %bitcast.212, bf16[1,1024,4,80]{1,3,2,0:T(8,128)(2,1)S(1)} %bitcast.210), kind=kOutput, calls=%fused_computation.149 | convolution fusion | flops 343933952 | bytes 9383936 | tf_op jit(solution)/shard_map/sub | solution.py:104
  137.7 5.0 %fusion.34 = bf16[4,80,512]{2,1,0:T(8,128)(2,1)S(1)} fusion(bf16[1024,4,80]{0,2,1:T(8,128)(2,1)S(1)} %bitcast.207, f32[4,512,1024]{2,1,0:T(8,128)} %get-tuple-element.13, f32[4,512]{1,0:T(4,128)S(1)} %get-tuple-element.12), kind=kOutput, calls=%fused_computation.54 | convolution fusion | flops 339902464 | bytes 9379840 | tf_op jit(solution)/shard_map/ihqk,ikhe->iqhe/dot_general | solution.py:105
  142.8 0.9 copy-done.13
  143.6 1.7 fusion.33
  145.3 4.0 %convolution_multiply_fusion = f32[1024,1280]{1,0:T(8,128)} fusion(bf16[320,1280]{0,1:T(8,128)(2,1)S(1)} %all_gather.16, f32[1024]{0:T(1024)S(1)} %bitcast.206, bf16[1,512,320]{1,2,0:T(8,128)(2,1)S(1)} %bitcast.214, bf16[1,512,320]{1,2,0:T(8,128)(2,1)S(1)} %bitcast.213), kind=kOutput, calls=%fused_computation.24 | convolution fusion | flops 841482240 | bytes 6721536 | tf_op jit(solution)/shard_map/ind,de->ine/dot_general | solution.py:110
  149.3 1.4 constant_dynamic-slice_fusion.2
  150.8 1.3 fusion.32
  152.0 3.1 %gather_fusion.1 = f32[16,1280]{1,0:T(8,128)S(1)} fusion(f32[1024,1280]{1,0:T(8,128)} %fusion.32, s32[1024]{0:T(1024)S(1)} %pad_clamp_fusion.1), kind=kCustom, calls=%fused_computation.1 | custom fusion | bytes 163904 | tf_op jit(solution)/shard_map/jit(take_along_axis)/gather | solution.py:19
  155.2 9.6 %gather_fusion = f32[1008,1280]{1,0:T(8,128)} fusion(f32[1024,1280]{1,0:T(8,128)} %fusion.32, s32[1024]{0:T(1024)S(1)} %pad_clamp_fusion.2), kind=kCustom, calls=%fused_computation | custom fusion | bytes 10325952 | tf_op jit(solution)/shard_map/jit(take_along_axis)/gather | solution.py:18
  164.7 5.5 %fusion.21 = bf16[1008,1,1280]{2,0,1:T(8,128)(2,1)S(1)} fusion(f32[1008,1280]{1,0:T(8,128)} %gather_fusion, pred[1008]{0:T(1024)(128)(4,1)S(1)} %compare_and_fusion, f32[16,1280]{1,0:T(8,128)S(1)} %gather_fusion.1, pred[16]{0:T(512)(128)(4,1)S(1)} %compare_and_fusion.1, s32[1008]{0:T(1024)S(1)} %bitcast.216, s32[16]{0:T(128)S(1)} %bitcast.226), kind=kOutput, calls=%fused_computation.34 | convolution fusion | flops 251633408 | bytes 7828480 | tf_op jit(solution)/shard_map/icr,ird->icd/dot_general | solution.py:21
  170.2 32.3 %fusion = bf16[256,1280]{1,0:T(8,128)(2,1)S(1)} fusion(bf16[1008,1,1280]{2,0,1:T(8,128)(2,1)S(1)} %fusion.21), kind=kCustom, calls=%all-reduce-scatter | all-reduce-scatter fusion | flops 1310721 | bytes 3236352
  202.6 4.4 %collective-permute-start.7 = (bf16[12,1280]{1,0:T(8,128)(2,1)S(1)}, bf16[12,1280]{1,0:T(8,128)(2,1)S(1)}, u32[]{:S(2)}, u32[]{:S(2)}) collective-permute-start(bf16[12,1280]{1,0:T(8,128)(2,1)S(1)} %slice.36), channel_id=1, source_target_pairs={{0,1},{1,2},{2,3},{4,5},{5,6},{6,7},{8,9},{9,10},{10,11},{12,13},{... | collective-permute-start | bytes 92168
  207.0 0.6 dynamic-slice.10
  208.3 1.3 concatenate.4
  210.9 2.1 copy.46
  213.1 39.8 %all-gather.7.cloned.1.call-done = bf16[1,1008,1280]{2,0,1:T(2,128)(2,1)} async-done(((bf16[1,252,1280]{2,0,1:T(2,128)(2,1)}), bf16[1,1008,1280]{2,0,1:T(2,128)(2,1)}) %all-gather.7.cloned.1.call-update) | async-done | bytes 2580496 | tf_op jit(solution)/shard_map/all_gather | solution.py:141
  253.0 12.9 %fusion.20 = bf16[1,1008,1280]{2,1,0:T(8,128)(2,1)} fusion(bf16[1280,1280]{0,1:T(8,128)(2,1)} %all-gather.11.cloned.1.call-done, bf16[1280,1280]{1,0:T(8,128)(2,1)} %all-gather.9.cloned.1.call-done, bf16[1,1008,1280]{2,0,1:T(2,128)(2,1)} %all-gather.7.cloned.1.call-done, f32[1280]{0:T(1024)S(1)} %copy-done.11), kind=kOutput, calls=%fused_computation.33 | convolution fusion | flops 6620221440 | bytes 11719680 | tf_op jit(solution)/shard_map/imf,fd->imd/dot_general | solution.py:150
  265.8 26.0 %fusion.1 = bf16[256,1280]{1,0:T(8,128)(2,1)S(1)} fusion(bf16[1,1008,1280]{2,1,0:T(8,128)(2,1)} %fusion.20), kind=kCustom, calls=%all-reduce-scatter.1 | all-reduce-scatter fusion | flops 1310721 | bytes 3236352
  291.9 4.4 %collective-permute-start.8 = (bf16[12,1280]{1,0:T(8,128)(2,1)S(1)}, bf16[12,1280]{1,0:T(8,128)(2,1)S(1)}, u32[]{:S(2)}, u32[]{:S(2)}) collective-permute-start(bf16[12,1280]{1,0:T(8,128)(2,1)S(1)} %slice.37), channel_id=1, source_target_pairs={{0,1},{1,2},{2,3},{4,5},{5,6},{6,7},{8,9},{9,10},{10,11},{12,13},{... | collective-permute-start | bytes 92168
  296.3 1.1 collective-permute-done.8
  297.4 1.0 concatenate.5
  298.4 1.3 add_convert_fusion.2
  (64 shorter events, 2.1 us)
Async XLA Ops:
  6.5 11.2 %copy-start.12 = (s32[1,16]{1,0:T(1,128)S(1)}, s32[1,16]{1,0:T(1,128)}, u32[]{:S(2)}) copy-start(s32[1,16]{1,0:T(1,128)} %param.21) | copy-start | bytes 196
  6.5 11.3 %copy-start = (f32[1,1024]{1,0:T(1,128)S(1)}, f32[1,1024]{1,0:T(1,128)}, u32[]{:S(2)}) copy-start(f32[1,1024]{1,0:T(1,128)} %param.13) | copy-start | bytes 12292
  6.5 11.3 %copy-start.7 = (s32[1,1008]{1,0:T(1,128)S(1)}, s32[1,1008]{1,0:T(1,128)}, u32[]{:S(2)}) copy-start(s32[1,1008]{1,0:T(1,128)} %param.23) | copy-start | bytes 12100
  6.5 13.5 %copy-start.9 = (s32[1,16]{1,0:T(1,128)S(1)}, s32[1,16]{1,0:T(1,128)}, u32[]{:S(2)}) copy-start(s32[1,16]{1,0:T(1,128)} %param.22) | copy-start | bytes 196
  6.5 42.3 %copy-start.6 = (bf16[320,160]{0,1:T(8,128)(2,1)S(1)}, bf16[320,160]{0,1:T(8,128)(2,1)}, u32[]{:S(2)}) copy-start(bf16[320,160]{0,1:T(8,128)(2,1)} %param.16) | copy-start | bytes 307204
  6.5 84.7 %all-gather.5.cloned.1.call-start = ((), (), s32[]{:S(2)}) async-start(), calls=%async_computation | async-start | bytes 3276800 | tf_op jit(solution)/shard_map/all_gather | solution.py:48
  11.6 201.5 %all-gather.11.cloned.1.call-start = ((), (), s32[]{:S(2)}) async-start(), calls=%async_computation.3 | async-start | bytes 3686400 | tf_op jit(solution)/shard_map/all_gather | solution.py:153
  12.3 200.8 %all-gather.9.cloned.1.call-start = ((), (), s32[]{:S(2)}) async-start(), calls=%async_computation.2 | async-start | bytes 3686400 | tf_op jit(solution)/shard_map/all_gather | solution.py:146
  12.4 17.6 %collective-permute-start.1 = (bf16[3,160,320]{2,1,0:T(8,128)(2,1)}, bf16[3,160,320]{2,1,0:T(8,128)(2,1)S(1)}, u32[]{:S(2)}, u32[]{:S(2)}) collective-permute-start(bf16[3,160,320]{2,1,0:T(8,128)(2,1)} %param.15), channel_id=1, source_target_pairs={{0,4},{4,8},{8,12},{12,16},{16,20},{20,24},{24,28},{28,0},{1,5},{5... | collective-permute-start | bytes 921608 | tf_op jit(solution)/shard_map/ppermute | solution.py:67
  14.5 17.7 %collective-permute-start = (bf16[3,160,320]{2,1,0:T(8,128)(2,1)}, bf16[3,160,320]{2,1,0:T(8,128)(2,1)S(1)}, u32[]{:S(2)}, u32[]{:S(2)}) collective-permute-start(bf16[3,160,320]{2,1,0:T(8,128)(2,1)} %param.15), channel_id=1, source_target_pairs={{0,28},{4,0},{8,4},{12,8},{16,12},{20,16},{24,20},{28,24},{1,29},{... | collective-permute-start | bytes 921608 | tf_op jit(solution)/shard_map/ppermute | solution.py:69
  17.6 235.4 %all-gather.7.cloned.1.call-start = ((), (), s32[]{:S(2)}) async-start(), calls=%async_computation.1 | async-start | bytes 6451200 | tf_op jit(solution)/shard_map/all_gather | solution.py:141
  30.0 16.7 %collective-permute-start.3 = (bf16[3,160,320]{2,1,0:T(8,128)(2,1)S(1)}, bf16[3,160,320]{2,1,0:T(8,128)(2,1)S(1)}, u32[]{:S(2)}, u32[]{:S(2)}) collective-permute-start(bf16[3,160,320]{2,1,0:T(8,128)(2,1)S(1)} %collective-permute-done.1), channel_id=1, source_target_pairs={{0,4},{4,8},{8,12},{12,16},{16,20},{20,24},{24,28},{28,0},{1,5},{5... | collective-permute-start | bytes 921608 | tf_op jit(solution)/shard_map/ppermute | solution.py:67
  32.2 62.2 %copy-start.4 = (bf16[3,160,320]{2,1,0:T(8,128)(2,1)}, bf16[3,160,320]{2,1,0:T(8,128)(2,1)S(1)}, u32[]{:S(2)}) copy-start(bf16[3,160,320]{2,1,0:T(8,128)(2,1)S(1)} %collective-permute-done) | copy-start | bytes 921604
  32.2 55.7 %collective-permute-start.2 = (bf16[3,160,320]{2,1,0:T(8,128)(2,1)S(1)}, bf16[3,160,320]{2,1,0:T(8,128)(2,1)}, u32[]{:S(2)}, u32[]{:S(2)}) collective-permute-start(bf16[3,160,320]{2,1,0:T(8,128)(2,1)S(1)} %collective-permute-done), channel_id=1, source_target_pairs={{0,28},{4,0},{8,4},{12,8},{16,12},{20,16},{24,20},{28,24},{1,29},{... | collective-permute-start | bytes 921608 | tf_op jit(solution)/shard_map/ppermute | solution.py:69
  46.7 44.6 %collective-permute-start.5 = (bf16[3,160,320]{2,1,0:T(8,128)(2,1)S(1)}, bf16[3,160,320]{2,1,0:T(8,128)(2,1)}, u32[]{:S(2)}, u32[]{:S(2)}) collective-permute-start(bf16[3,160,320]{2,1,0:T(8,128)(2,1)S(1)} %collective-permute-done.3), channel_id=1, source_target_pairs={{0,4},{4,8},{8,12},{12,16},{16,20},{20,24},{24,28},{28,0},{1,5},{5... | collective-permute-start | bytes 921608 | tf_op jit(solution)/shard_map/ppermute | solution.py:67
  87.9 27.6 %collective-permute-start.4 = (bf16[3,160,320]{2,1,0:T(8,128)(2,1)}, bf16[3,160,320]{2,1,0:T(8,128)(2,1)}, u32[]{:S(2)}, u32[]{:S(2)}) collective-permute-start(bf16[3,160,320]{2,1,0:T(8,128)(2,1)} %collective-permute-done.2), channel_id=1, source_target_pairs={{0,28},{4,0},{8,4},{12,8},{16,12},{20,16},{24,20},{28,24},{1,29},{... | collective-permute-start | bytes 921608 | tf_op jit(solution)/shard_map/ppermute | solution.py:69
  91.3 27.9 %collective-permute-start.6 = (bf16[3,160,320]{2,1,0:T(8,128)(2,1)}, bf16[3,160,320]{2,1,0:T(8,128)(2,1)}, u32[]{:S(2)}, u32[]{:S(2)}) collective-permute-start(bf16[3,160,320]{2,1,0:T(8,128)(2,1)} %collective-permute-done.5), channel_id=1, source_target_pairs={{0,4},{4,8},{8,12},{12,16},{16,20},{20,24},{24,28},{28,0},{1,5},{5... | collective-permute-start | bytes 921608 | tf_op jit(solution)/shard_map/ppermute | solution.py:67
  91.3 2.2 copy-start.2
  96.2 1.0 copy-start.5
  96.2 1.8 copy-start.3
  137.7 5.9 %copy-start.13 = (f32[4,512,1024]{2,1,0:T(8,128)S(1)}, f32[4,512,1024]{2,1,0:T(8,128)}, u32[]{:S(2)}) copy-start(f32[4,512,1024]{2,1,0:T(8,128)} %get-tuple-element.11) | copy-start | bytes 25165828
  145.3 5.4 %copy-start.1 = (bf16[1,256,1280]{2,1,0:T(8,128)(2,1)S(1)}, bf16[1,256,1280]{2,1,0:T(8,128)(2,1)}, u32[]{:S(2)}) copy-start(bf16[1,256,1280]{2,1,0:T(8,128)(2,1)} %param.12) | copy-start | bytes 1966084
  164.7 42.3 %copy-start.10 = (u32[32]{0:T(128)S(1)}, u32[32]{0:T(128)}, u32[]{:S(2)}) copy-start(u32[32]{0:T(128)} %constant.159) | copy-start | bytes 388
  170.2 40.3 %copy-start.8 = (f32[1280]{0:T(1024)S(1)}, f32[1280]{0:T(1024)}, u32[]{:S(2)}) copy-start(f32[1280]{0:T(1024)} %param.17) | copy-start | bytes 15364
  202.6 50.4 %copy-start.11 = (f32[1280]{0:T(1024)S(1)}, f32[1280]{0:T(1024)}, u32[]{:S(2)}) copy-start(f32[1280]{0:T(1024)} %param.19) | copy-start | bytes 15364
  202.6 5.7 %collective-permute-start.7 = (bf16[12,1280]{1,0:T(8,128)(2,1)S(1)}, bf16[12,1280]{1,0:T(8,128)(2,1)S(1)}, u32[]{:S(2)}, u32[]{:S(2)}) collective-permute-start(bf16[12,1280]{1,0:T(8,128)(2,1)S(1)} %slice.36), channel_id=1, source_target_pairs={{0,1},{1,2},{2,3},{4,5},{5,6},{6,7},{8,9},{9,10},{10,11},{12,13},{... | collective-permute-start | bytes 92168
  291.9 5.5 %collective-permute-start.8 = (bf16[12,1280]{1,0:T(8,128)(2,1)S(1)}, bf16[12,1280]{1,0:T(8,128)(2,1)S(1)}, u32[]{:S(2)}, u32[]{:S(2)}) collective-permute-start(bf16[12,1280]{1,0:T(8,128)(2,1)S(1)} %slice.37), channel_id=1, source_target_pairs={{0,1},{1,2},{2,3},{4,5},{5,6},{6,7},{8,9},{9,10},{10,11},{12,13},{... | collective-permute-start | bytes 92168
Sparse Core Ops, SparseCore 0:
  11.7 27.9 all-gather.4
  41.9 91.1 all-gather.10
  135.3 59.7 all-gather.8
  213.2 39.7 all-gather.6
